TPU v7x, 32 devices: a whole 2x2x4 slice. The times are simulated.
32 devices in a mesh: grow: 4 (over y, x), gcol: 8 (over z, core).
Axes of the slice: x: 2, y: 2, z: 4, core: 2. Of those that a mesh axis runs over, the one named last changes fastest.
Arguments:
- psi: float32 [32768, 1024], P(('grow', 'gcol')), may hold values from -6 to 6
- vpsi: float32 [32768, 1024], P(('grow', 'gcol')), may hold values from -6 to 6
- kinetic: float32 [32768], P(('grow', 'gcol')), may hold values from 0.1 to 10
- mixing: float32 [1024, 1024], P('grow', 'gcol'), may hold values from -0.1875 to 0.1875
Outputs:
- residual: float32 [32768, 1024], P(('grow', 'gcol'))
- projected: float32 [1024, 1024], P('grow', 'gcol')
All inputs are finite; a program needn't handle non-finite values.
Results may differ from a plain program's by a relative error of at most 0.000073.
Values sent between devices are 32-bit elements; how exact they have to be, the bound alone decides.
A program may use at most 128 MiB of HBM per device.

v0:
```python
import jax
import jax.numpy as jnp
from jax import lax
from jax.sharding import PartitionSpec as P


def body(psi, vpsi, kinetic, mixing):
    n_grow = lax.axis_size("grow")
    n_gcol = lax.axis_size("gcol")
    bands = psi.shape[1]
    scale = 1.0 / (psi.shape[0] * n_grow * n_gcol)
    hpsi = kinetic[:, None] * psi + vpsi
    block_rows = bands // n_grow
    block_cols = bands // n_gcol
    partial_value = (
        lax.dot_general(
            psi,
            hpsi,
            (((0,), (0,)), ((), ())),
            precision=lax.Precision.HIGHEST,
            preferred_element_type=jnp.float32,
        )
        * scale
    )
    full = lax.psum(partial_value, ("grow", "gcol"))
    row_start = lax.axis_index("grow") * block_rows
    col_start = lax.axis_index("gcol") * block_cols
    projected = lax.dynamic_slice(full, (row_start, col_start), (block_rows, block_cols))
    correction = hpsi - jnp.dot(
        psi, full, precision=lax.Precision.HIGHEST, preferred_element_type=jnp.float32
    )
    mix_panel = lax.all_gather(mixing, "gcol", axis=1, tiled=True)
    residual = jnp.dot(
        correction,
        lax.all_gather(mix_panel, "grow", axis=0, tiled=True),
        precision=lax.Precision.HIGHEST,
        preferred_element_type=jnp.float32,
    )
    return (residual, projected)


def solution(mesh):
    return jax.shard_map(
        body,
        mesh=mesh,
        in_specs=(
            P(("grow", "gcol"), None),
            P(("grow", "gcol"), None),
            P(("grow", "gcol")),
            P("grow", "gcol"),
        ),
        out_specs=(P(("grow", "gcol"), None), P("grow", "gcol")),
        check_vma=False,
    )
```

profile of v0, /device:TPU:0, one launch (start us, length us, event | category | flops | bytes accessed | tf_op | source)
XLA Modules:
  0.0 237.2 jit_solution(7438107211966366127)
XLA Ops:
  8.0 0.0 all-gather.3.cloned.1.call-start
  8.0 0.7 all-gather.3.cloned.1.call-update
  8.7 0.0 all-reduce.2.cloned.1.call-start
  8.8 18.8 %multiply_bitcast_fusion = f32[1024,1024]{0,1:T(8,128)} fusion(f32[1024,1024]{1,0:T(8,128)} %param.4, f32[1024,1024]{1,0:T(8,128)} %param.5, f32[1024]{0:T(1024)} %param.6), kind=kOutput, calls=%fused_computation.2 | convolution fusion | flops 12888047616 | bytes 12587008 | tf_op jit(solution)/shard_map/dot_general | solution.py:16
  27.5 0.0 all-reduce.2.cloned.1.call-update
  27.6 0.2 all-gather.5.cloned.1.call-start
  27.8 9.2 %all-gather.3.cloned.1.call-done = f32[256,1024]{1,0:T(8,128)} async-done(((f32[256,128]{1,0:T(8,128)}), f32[256,1024]{1,0:T(8,128)}) %all-gather.3.cloned.1.call-update) | async-done | bytes 1048592 | tf_op jit(solution)/shard_map/all_gather | solution.py:32
  37.0 0.0 all-gather.5.cloned.1.call-update
  37.1 154.0 %all-reduce.2.cloned.1.call-done = f32[1024,1024]{0,1:T(8,128)} async-done(((f32[1024,1024]{0,1:T(8,128)}), f32[1024,1024]{0,1:T(8,128)}) %all-reduce.2.cloned.1.call-update) | async-done | bytes 4194320 | tf_op jit(solution)/shard_map/psum | solution.py:25
  191.1 0.9 dynamic_slice.3
  192.0 0.8 copy.6
  192.7 0.0 copy-start
  192.7 17.7 %fusion.4 = f32[1024,1024]{0,1:T(8,128)} fusion(f32[1024,1024]{0,1:T(8,128)} %all-reduce.2.cloned.1.call-done, f32[1024,1024]{1,0:T(8,128)} %param.4), kind=kOutput, calls=%fused_computation.7 | convolution fusion | flops 12884901888 | bytes 12582912 | tf_op jit(solution)/shard_map/dot_general | solution.py:29
  210.5 0.0 all-gather.5.cloned.1.call-done
  210.5 0.0 copy-done
  210.5 19.3 %fusion = f32[1024,1024]{1,0:T(8,128)} fusion(f32[1024,1024]{1,0:T(8,128)} %all-gather.5.cloned.1.call-done, f32[1024,1024]{0,1:T(8,128)} %fusion.4, f32[1024,1024]{1,0:T(8,128)} %param.5, f32[1024,1024]{1,0:T(8,128)} %param.4, f32[1024]{0:T(1024)S(1)} %copy-done), kind=kOutput, calls=%fused_computation.1 | convolution fusion | flops 12888047616 | bytes 20975616 | tf_op jit(solution)/shard_map/dot_general | solution.py:33
Async XLA Ops:
  8.0 29.0 %all-gather.3.cloned.1.call-start = ((), (), s32[]{:S(2)}) async-start(), calls=%async_computation.1 | async-start | bytes 1179648 | tf_op jit(solution)/shard_map/all_gather | solution.py:32
  8.7 182.3 %all-reduce.2.cloned.1.call-start = ((), (), s32[]{:S(2)}) async-start(), calls=%async_computation | async-start | bytes 8388608 | tf_op jit(solution)/shard_map/psum | solution.py:25
  27.6 182.9 %all-gather.5.cloned.1.call-start = ((), (), s32[]{:S(2)}) async-start(), calls=%async_computation.2 | async-start | bytes 5242880 | tf_op jit(solution)/shard_map/all_gather | solution.py:35
  192.7 17.7 %copy-start = (f32[1024]{0:T(1024)S(1)}, f32[1024]{0:T(1024)}, u32[]{:S(2)}) copy-start(f32[1024]{0:T(1024)} %param.6) | copy-start | bytes 12292
Sparse Core Ops, SparseCore 0:
  10.4 26.6 all-gather.2
  38.9 52.5 all-gather.4
Sparse Core Ops, SparseCore 1:
  27.6 163.4 all-reduce.1
where the time goes:
time: 237 us
  waiting for transfers between devices  164 us (69%)
  matrix products  55.8 us (24%)
  between operations  15.5 us (7%)
    psum x1, waiting for transfers between devices, body(): full = lax.psum(partial_value, ('grow', 'gcol'))  154 us
    dot_general x1, matrix products, body(): jnp.dot(correction, lax.all_gather(mix_panel, 'grow', axis=0, tiled=True)...  19.3 us
    dot_general x1, matrix products, body(): lax.dot_general(psi, hpsi, (((0,), (0,)), ((), ())), precision=lax.Precis...  18.8 us
    dot_general x1, matrix products, body(): jnp.dot(psi, full, precision=lax.Precision.HIGHEST, preferred_element_typ...  17.7 us
    all_gather x1, waiting for transfers between devices, body(): mix_panel = lax.all_gather(mixing, 'gcol', axis=1, tiled=True)  9.25 us
  transfers between devices with their start and end apart: 3, of which 2 were waited for; matrix products, arithmetic and copies ran while one was open for 16% of the time, Pallas kernels for 0%

commit v1 on v0

v1 whole, which is shorter than its diff:
```python
import functools

import jax
import jax.numpy as jnp
from jax import lax
from jax.experimental import pallas as pl
from jax.experimental.pallas import tpu as pltpu
from jax.sharding import PartitionSpec as P

F32 = jnp.float32
BF16 = jnp.bfloat16
TN = 256


def split(x):
    hi = x.astype(BF16)
    return hi, (x - hi.astype(F32)).astype(BF16)


def dot3(ah, al, bh, bl):
    dot = functools.partial(jnp.dot, preferred_element_type=F32)
    return dot(ah, bh) + (dot(ah, bl) + dot(al, bh))


def kernel(nz, scale, psi_hbm, vpsi_hbm, kin_ref, mix_ref, res_ref, proj_ref,
           psi_v, vpsi_v, psh, psl, pth, ptl, hh, hl, mh, ml, part, r0, r1, r2,
           rzr, rzl, mg, q, pown, pin,
           ld, m1s, m1r, m2s, m2r, mzs, mzr, mcs, mcr, mloc,
           s0s, s0r, s1s, s1r, s2s, s2r, zs, zrr, zrl, ps, pr, ploc,
           qzs, qzr, q2s, q2r, q1s, q1r, qcs, qcr):
    rows, nb = psi_v.shape
    n_grow = mg.shape[1]
    n_gcol = mg.shape[0]
    each = part.shape[4]
    bc = nb // n_gcol
    br = nb // n_grow
    half = br // 2
    grp = 2 * half
    g = lax.axis_index("grow")
    gc = lax.axis_index("gcol")
    z = gc // 2
    core = gc % 2
    pc = 1 - core
    w1 = 1 + core
    w2 = 2 - core
    a = (g // w1) % 2
    b = (g // w2) % 2
    ap, bp = b, a
    g1 = g + w1 * (1 - 2 * a)
    g2 = g + w2 * (1 - 2 * b)
    dev_c = {"grow": g, "gcol": z * 2 + pc}
    dev_1 = {"grow": g1, "gcol": gc}
    dev_2 = {"grow": g2, "gcol": gc}
    dev_r = {"grow": g, "gcol": lax.rem(gc + 2, n_gcol)}
    dev_l = {"grow": g, "gcol": lax.rem(gc + n_gcol - 2, n_gcol)}

    def rc(src, dst, ss, rs, dev):
        return pltpu.make_async_remote_copy(
            src_ref=src, dst_ref=dst, send_sem=ss, recv_sem=rs,
            device_id=dev, device_id_type=pl.DeviceIdType.MESH)

    nch = ld.shape[1]
    ch = rows // nch

    def loads(i):
        s = pl.ds(i * ch, ch)
        return (pltpu.make_async_copy(psi_hbm.at[s], psi_v.at[s], ld.at[0, i]),
                pltpu.make_async_copy(vpsi_hbm.at[s], vpsi_v.at[s], ld.at[1, i]))

    for i in range(nch):
        for c in loads(i):
            c.start()
    own_m = pltpu.make_async_copy(mix_ref, mg.at[gc, g], mloc)
    own_m.start()

    barrier = pltpu.get_barrier_semaphore()
    for k in range(1, n_gcol):
        pl.semaphore_signal(barrier, inc=1, device_id={"grow": g, "gcol": lax.rem(gc + k, n_gcol)},
                            device_id_type=pl.DeviceIdType.MESH)
    for dev in (dev_1, dev_2):
        pl.semaphore_signal(barrier, inc=1, device_id=dev, device_id_type=pl.DeviceIdType.MESH)
    pl.semaphore_wait(barrier, n_gcol - 1 + 2)

    m_1 = rc(mix_ref, mg.at[gc, g], m1s, m1r, dev_1)
    m_1.start()

    kt = jnp.transpose(jnp.broadcast_to(kin_ref[...], (128, rows)))
    for i in range(nch):
        for c in loads(i):
            c.wait()
        r = slice(i * ch, (i + 1) * ch)
        for cc in range(2):
            for ba in range(2):
                for bb in range(2):
                    gg = (ba + 2 * bb) if cc == 0 else (2 * ba + bb)
                    for s in range(0, half, 128):
                        col = gg * br + cc * half + s
                        x = psi_v[r, col:col + 128]
                        h = kt[r, :] * x + vpsi_v[r, col:col + 128]
                        hhi, hlo = split(h)
                        hh[r, col:col + 128] = hhi
                        hl[r, col:col + 128] = hlo
                        xhi, xlo = split(x)
                        o = bb * half + s
                        k = cc * 2 + ba
                        psh[k, r, o:o + 128] = xhi
                        psl[k, r, o:o + 128] = xlo
                        pth[k, o:o + 128, r] = jnp.transpose(xhi)
                        ptl[k, o:o + 128, r] = jnp.transpose(xlo)

    own_m.wait()
    m_1.wait()
    mg_1 = [rc(mg.at[gc, gx], mg.at[gc, gx], m2s.at[k], m2r.at[k], dev_2)
            for k, gx in enumerate((g, g1))]
    for c in mg_1:
        c.start()

    def mm1(cx, ax):
        k = cx * 2 + ax

        @pl.loop(0, nb // TN)
        def _(j):
            n = pl.ds(pl.multiple_of(j * TN, TN), TN)
            out = dot3(pth[k], ptl[k], hh[:, n], hl[:, n])
            part[cx, ax, :, :, :, n] = out.reshape(2, nz, each, TN)

    def line(at, ss, rs):
        def right(t):
            return rc(at(z - t), at(z - t), ss.at[0, t], rs.at[z - t], dev_r)

        def left(t):
            return rc(at(z + t), at(z + t), ss.at[1, t], rs.at[z + t], dev_l)

        def step(t):
            @pl.when(z - t >= 0)
            def _():
                if t > 0:
                    rc(at(z - t), at(z - t), ss.at[0, 0], rs.at[z - t], dev_r).wait_recv()

                @pl.when(z < nz - 1)
                def _():
                    if t < nz - 1:
                        right(t).start()

            @pl.when(z + t < nz)
            def _():
                if t > 0:
                    rc(at(z + t), at(z + t), ss.at[1, 0], rs.at[z + t], dev_l).wait_recv()

                @pl.when(z > 0)
                def _():
                    if t < nz - 1:
                        left(t).start()

        def drain():
            for t in range(nz - 1):
                @pl.when((z - t >= 0) & (z < nz - 1))
                def _():
                    right(t).wait_send()

                @pl.when((z + t < nz) & (z > 0))
                def _():
                    left(t).wait_send()

        return step, drain

    m_step, m_drain = line(lambda i: mg.at[2 * i + core], mzs, mzr)

    s0 = []
    for i, ax in enumerate((1 - ap, ap)):
        mm1(pc, ax)
        c = rc(part.at[pc, ax], r0.at[i], s0s.at[i], s0r.at[i], dev_c)
        c.start()
        s0.append(c)
        if i == 0:
            for c in mg_1:
                c.wait()
            m_step(0)

    mm1(core, 1 - a)
    s0[0].wait_recv()
    s1 = []
    for i, bx in enumerate((1 - b, b)):
        part[core, 1 - a, bx] = part[core, 1 - a, bx] + r0[0, bx]
        c = rc(part.at[core, 1 - a, bx], r1.at[i], s1s.at[i], s1r.at[i], dev_1)
        c.start()
        s1.append(c)
    mm1(core, a)
    s0[1].wait_recv()
    for bx in range(2):
        part[core, a, bx] = part[core, a, bx] + r0[1, bx]
    m_step(1)
    s1[0].wait_recv()
    part[core, a, 1 - b] = part[core, a, 1 - b] + r1[0]
    s2 = rc(part.at[core, a, 1 - b], r2, s2s, s2r, dev_2)
    s2.start()
    s1[1].wait_recv()
    part[core, a, b] = part[core, a, b] + r1[1]
    for t in range(2, nz - 1):
        m_step(t)
    s2.wait_recv()
    part[core, a, b] = part[core, a, b] + r2[...]

    def zr(t):
        d = nz - 1 - t
        return rc(part.at[core, a, b, d], rzr.at[d], zs.at[0, t], zrr.at[d], dev_r)

    def zl(t):
        return rc(part.at[core, a, b, t], rzl.at[t], zs.at[1, t], zrl.at[t], dev_l)

    for t in range(nz):
        d = nz - 1 - t

        @pl.when((z > 0) & (d >= z))
        def _():
            rc(part.at[core, a, b, d], rzr.at[d], zs.at[0, 0], zrr.at[d], dev_r).wait_recv()
            part[core, a, b, d] = part[core, a, b, d] + rzr[d]

        if t < nz - 1:
            @pl.when(d > z)
            def _():
                zr(t).start()

        @pl.when((z < nz - 1) & (t <= z))
        def _():
            rc(part.at[core, a, b, t], rzl.at[t], zs.at[1, 0], zrl.at[t], dev_l).wait_recv()
            part[core, a, b, t] = part[core, a, b, t] + rzl[t]

        if t < nz - 1:
            @pl.when(t < z)
            def _():
                zl(t).start()

    own = part[core, a, b, z] * scale
    pown[...] = own
    for k in range(n_gcol):
        pin_k = own[:, k * bc:(k + 1) * bc]
        pin[k] = pin_k
    sends = []
    row0 = pl.multiple_of(core * half + z * each, each)
    for k in range(1, n_gcol):
        to = lax.rem(gc + k, n_gcol)
        c = rc(pin.at[to], proj_ref.at[pl.ds(row0, each)], ps.at[k], pr.at[k],
               {"grow": g, "gcol": to})
        c.start()
        sends.append(c)
    own_p = pltpu.make_async_copy(pin.at[gc], proj_ref.at[pl.ds(row0, each)], ploc)
    own_p.start()

    m_step(nz - 1)
    mc = []
    for i in range(nz):
        c = rc(mg.at[2 * i + core], mg.at[2 * i + core], mcs.at[i], mcr.at[i], dev_c)
        c.start()
        mc.append(c)
    for i in range(nz):
        rc(mg.at[2 * i + pc], mg.at[2 * i + pc], mcs.at[i], mcr.at[i], dev_c).wait_recv()

    @pl.loop(0, n_gcol)
    def _(k):
        n = pl.ds(pl.multiple_of(k * bc, bc), bc)
        for gx in range(n_grow):
            hi, lo = split(mg[k, gx])
            mh[gx * br:(gx + 1) * br, n] = hi
            ml[gx * br:(gx + 1) * br, n] = lo

    ph, plo = split(pown[...])

    @pl.loop(0, nb // TN)
    def _(j):
        n = pl.ds(pl.multiple_of(j * TN, TN), TN)
        q[core, a, b, z, :, n] = dot3(ph, plo, mh[:, n], ml[:, n])

    q_step, q_drain = line(lambda i: q.at[core, a, b, i], qzs, qzr)

    def hmix(i):
        @pl.loop(0, nb // TN)
        def _(j):
            n = pl.ds(pl.multiple_of(j * TN, TN), TN)
            r = slice(i * (rows // 4), (i + 1) * (rows // 4))
            res_ref[r, n] = dot3(hh[r, :], hl[r, :], mh[:, n], ml[:, n])

    def finish(cx, ax):
        k = cx * 2 + ax

        @pl.loop(0, nb // TN)
        def _(j):
            n = pl.ds(pl.multiple_of(j * TN, TN), TN)
            qh, ql = split(q[cx, ax, :, :, :, n].reshape(grp, TN))
            for i in range(4):
                r = slice(i * (rows // 4), (i + 1) * (rows // 4))
                res_ref[r, n] = res_ref[r, n] - dot3(psh[k, r, :], psl[k, r, :], qh, ql)

    def qc(i, cx, ax, bx):
        return rc(q.at[cx, ax, bx], q.at[cx, ax, bx], qcs.at[i], qcr.at[i], dev_c)

    mine = ((a, b), (a, 1 - b), (1 - a, b), (1 - a, 1 - b))
    other = ((ap, bp), (ap, 1 - bp), (1 - ap, bp), (1 - ap, 1 - bp))

    q_step(0)
    hmix(0)
    for t in range(1, nz):
        q_step(t)
        if t < min(4, nz - 1):
            hmix(t)
    q2 = rc(q.at[core, a, b], q.at[core, a, b], q2s, q2r, dev_2)
    q2.start()
    q1 = [rc(q.at[core, a, b], q.at[core, a, b], q1s.at[0], q1r.at[0], dev_1),
          rc(q.at[core, a, 1 - b], q.at[core, a, 1 - b], q1s.at[1], q1r.at[1], dev_1)]
    q1[0].start()
    qc(0, core, *mine[0]).start()
    for i in range(min(4, nz - 1), 4):
        hmix(i)
    rc(q.at[core, a, 1 - b], q.at[core, a, 1 - b], q2s, q2r, dev_2).wait_recv()
    q1[1].start()
    qc(1, core, *mine[1]).start()
    finish(core, a)
    qc(0, pc, *other[0]).wait_recv()
    qc(1, pc, *other[1]).wait_recv()
    finish(pc, ap)
    rc(q.at[core, 1 - a, b], q.at[core, 1 - a, b], q1s.at[0], q1r.at[0], dev_1).wait_recv()
    qc(2, core, *mine[2]).start()
    rc(q.at[core, 1 - a, 1 - b], q.at[core, 1 - a, 1 - b], q1s.at[1], q1r.at[1], dev_1).wait_recv()
    qc(3, core, *mine[3]).start()
    finish(core, 1 - a)
    qc(2, pc, *other[2]).wait_recv()
    qc(3, pc, *other[3]).wait_recv()
    finish(pc, 1 - ap)

    for k in range(1, n_gcol):
        src = lax.rem(gc + n_gcol - k, n_gcol)
        r_src = pl.multiple_of((src % 2) * half + (src // 2) * each, each)
        rc(pin.at[src], proj_ref.at[pl.ds(r_src, each)], ps.at[k], pr.at[k],
           {"grow": g, "gcol": src}).wait_recv()
        sends[k - 1].wait_send()
    own_p.wait()
    for c in mc + s0 + s1 + [s2, q2] + q1:
        c.wait_send()
    for i in range(4):
        qc(i, core, *mine[i]).wait_send()
    m_drain()
    q_drain()
    for t in range(nz - 1):
        @pl.when(nz - 1 - t > z)
        def _():
            zr(t).wait_send()

        @pl.when(t < z)
        def _():
            zl(t).wait_send()


def body_kernel(psi, vpsi, kinetic, mixing):
    n_grow = lax.axis_size("grow")
    n_gcol = lax.axis_size("gcol")
    rows, nb = psi.shape
    nz = n_gcol // 2
    each = nb // (n_grow * n_gcol)
    br, bc = nb // n_grow, nb // n_gcol
    scale = 1.0 / (rows * n_grow * n_gcol)
    D = pltpu.SemaphoreType.DMA
    nch = 4
    grp = nb // 4
    V = pltpu.VMEM
    return pl.pallas_call(
        functools.partial(kernel, nz, scale),
        out_shape=(jax.ShapeDtypeStruct((rows, nb), F32), jax.ShapeDtypeStruct((br, bc), F32)),
        in_specs=[pl.BlockSpec(memory_space=pl.ANY), pl.BlockSpec(memory_space=pl.ANY),
                  pl.BlockSpec(memory_space=pltpu.VMEM), pl.BlockSpec(memory_space=pltpu.VMEM)],
        out_specs=(pl.BlockSpec(memory_space=pltpu.VMEM), pl.BlockSpec(memory_space=pltpu.VMEM)),
        scratch_shapes=[
            V((rows, nb), F32), V((rows, nb), F32),
            V((4, rows, grp), BF16), V((4, rows, grp), BF16),
            V((4, grp, rows), BF16), V((4, grp, rows), BF16),
            V((rows, nb), BF16), V((rows, nb), BF16),
            V((nb, nb), BF16), V((nb, nb), BF16),
            V((2, 2, 2, nz, each, nb), F32), V((2, 2, nz, each, nb), F32),
            V((2, nz, each, nb), F32), V((nz, each, nb), F32),
            V((nz, each, nb), F32), V((nz, each, nb), F32),
            V((n_gcol, n_grow, br, bc), F32),
            V((2, 2, 2, nz, each, nb), F32),
            V((each, nb), F32), V((n_gcol, each, bc), F32),
            D((2, nch)), D, D, D((2,)), D((2,)), D((2, nz)), D((nz,)), D((nz,)), D((nz,)), D,
            D((2,)), D((2,)), D((2,)), D((2,)), D, D, D((2, nz)), D((nz,)), D((nz,)),
            D((n_gcol,)), D((n_gcol,)), D,
            D((2, nz)), D((nz,)), D, D, D((2,)), D((2,)), D((4,)), D((4,)),
        ],
        compiler_params=pltpu.CompilerParams(
            collective_id=0, has_side_effects=True, vmem_limit_bytes=67043328),
    )(psi, vpsi, kinetic.reshape(1, rows), mixing)


def body_plain(psi, vpsi, kinetic, mixing):
    n_grow = lax.axis_size("grow")
    n_gcol = lax.axis_size("gcol")
    bands = psi.shape[1]
    scale = 1.0 / (psi.shape[0] * n_grow * n_gcol)
    dot = functools.partial(
        lax.dot_general, precision=lax.Precision.HIGHEST, preferred_element_type=F32)
    hpsi = kinetic[:, None] * psi + vpsi
    full = lax.psum(dot(psi, hpsi, (((0,), (0,)), ((), ()))) * scale, ("grow", "gcol"))
    panel = lax.all_gather(mixing, "gcol", axis=1, tiled=True)
    mix = lax.all_gather(panel, "grow", axis=0, tiled=True)
    br, bc = bands // n_grow, bands // n_gcol
    projected = lax.dynamic_slice(
        full, (lax.axis_index("grow") * br, lax.axis_index("gcol") * bc), (br, bc))
    last = (((1,), (0,)), ((), ()))
    residual = dot(hpsi - dot(psi, full, last), mix, last)
    return residual, projected


def body(psi, vpsi, kinetic, mixing):
    n_grow = lax.axis_size("grow")
    n_gcol = lax.axis_size("gcol")
    rows, nb = psi.shape
    fits = (n_grow == 2 * 2 and n_gcol % 2 == 0 and nb % (8 * n_grow * n_gcol) == 0
            and (nb // n_gcol) % 128 == 0 and (nb // n_grow) % 256 == 0 and rows % 512 == 0)
    return (body_kernel if fits else body_plain)(psi, vpsi, kinetic, mixing)


def solution(mesh):
    return jax.shard_map(
        body,
        mesh=mesh,
        in_specs=(
            P(("grow", "gcol"), None),
            P(("grow", "gcol"), None),
            P(("grow", "gcol")),
            P("grow", "gcol"),
        ),
        out_specs=(P(("grow", "gcol"), None), P("grow", "gcol")),
        check_vma=False,
    )
```

time: 237 us -> 129 us (0.54)
  waiting for transfers between devices: 164 us -> 0 us
  Pallas kernels: 0 us -> 123 us
  matrix products: 55.8 us -> 0 us
  between operations: 15.5 us -> 0.65 us
  local copies, waits for them, and re-layouts: 1.67 us -> 5.48 us
    psum x1 -> x0, waiting for transfers between devices: 154 us -> none  [body(): full = lax.psum(partial_value, ('grow', 'gcol'))]
    pallas_call x0 -> x1, Pallas kernels: none -> 123 us  [body_kernel(): pl.pallas_call(functools.partial(kernel, nz, scale), out_shape=(jax.Shape...]
    dot_general x3 -> x0, matrix products: 55.8 us -> none  [the longest x1 19.3 us: body(): jnp.dot(correction, lax.all_gather(mix_panel, 'grow', axis=0, tiled=True)...]
    all_gather x2 -> x0, waiting for transfers between devices: 9.25 us -> none  [the longest x1 9.25 us: body(): mix_panel = lax.all_gather(mixing, 'gcol', axis=1, tiled=True)]
    unnamed x3 -> x4, local copies, waits for them, and re-layouts: 0.76 us -> 5.48 us
  transfers between devices with their start and end apart: 3 -> 0, of which waited for: 2 -> 0; matrix products, arithmetic and copies ran while one was open for 16% -> 0% of each run, Pallas kernels for 0% -> 0%
where the time goes in v1:
time: 129 us
  Pallas kernels  123 us (95%)
  local copies, waits for them, and re-layouts  5.48 us (4%)
    pallas_call x1, Pallas kernels, body_kernel(): pl.pallas_call(functools.partial(kernel, nz, scale), out_shape=(jax.Shape...  123 us
    unnamed x4, local copies, waits for them, and re-layouts  5.48 us

profile of v1, /device:TPU:0, one launch (start us, length us, event | category | flops | bytes accessed | tf_op | source)
XLA Modules:
  0.0 128.8 jit_solution(8998299758855147175)
XLA Ops:
  0.6 122.6 %shard_map.59 = (f32[1024,1024]{1,0:T(8,128)}, f32[256,128]{1,0:T(8,128)}) custom-call(f32[1024,1024]{1,0:T(8,128)} %psi_hbm.1, f32[1024,1024]{1,0:T(8,128)} %vpsi_hbm.1, f32[1,1024]{1,0:T(1,128)} %bitcast.1, f32[256,128]{1,0:T(8,128)} %mix_ref.1), custom_call_target="tpu_custom_call" | custom-call | tf_op jit(solution)/shard_map/pallas_call | solution.py:365
  123.3 0.0 copy-start
  123.3 4.8 %copy.8 = f32[1024,1024]{1,0:T(8,128)} copy(f32[1024,1024]{1,0:T(8,128)} %get-tuple-element.4) | data formatting | bytes 8388608
  128.1 0.0 copy-done
  128.1 0.7 copy.9
Async XLA Ops:
  123.3 4.8 %copy-start = (f32[256,128]{1,0:T(8,128)S(1)}, f32[256,128]{1,0:T(8,128)}, u32[]{:S(2)}) copy-start(f32[256,128]{1,0:T(8,128)} %get-tuple-element.5) | copy-start | bytes 393220

commit v2 on v1

--- a/solution.py
+++ b/solution.py
@@ -24,13 +24,14 @@
 
 def kernel(nz, scale, psi_hbm, vpsi_hbm, kin_ref, mix_ref, res_ref, proj_ref,
            psi_v, vpsi_v, psh, psl, pth, ptl, hh, hl, mh, ml, part, r0, r1, r2,
-           rzr, rzl, mg, q, pown, pin,
-           ld, m1s, m1r, m2s, m2r, mzs, mzr, mcs, mcr, mloc,
+           rzr, rzl, ma, mb, q, pown, pin,
+           ld, mloc, azs, azr, a1s, a1r, a2s, a2r, b1s, b1r, b2s, b2r, bzs, bzr,
+           mcs, mcr,
            s0s, s0r, s1s, s1r, s2s, s2r, zs, zrr, zrl, ps, pr, ploc,
            qzs, qzr, q2s, q2r, q1s, q1r, qcs, qcr):
     rows, nb = psi_v.shape
-    n_grow = mg.shape[1]
-    n_gcol = mg.shape[0]
+    n_grow = mb.shape[2]
+    n_gcol = 2 * nz
     each = part.shape[4]
     bc = nb // n_gcol
     br = nb // n_grow
@@ -59,6 +60,46 @@
             src_ref=src, dst_ref=dst, send_sem=ss, recv_sem=rs,
             device_id=dev, device_id_type=pl.DeviceIdType.MESH)
 
+    def line(at, ss, rs):
+        def right(t):
+            return rc(at(z - t), at(z - t), ss.at[0, t], rs.at[z - t], dev_r)
+
+        def left(t):
+            return rc(at(z + t), at(z + t), ss.at[1, t], rs.at[z + t], dev_l)
+
+        def step(t):
+            @pl.when(z - t >= 0)
+            def _():
+                if t > 0:
+                    rc(at(z - t), at(z - t), ss.at[0, 0], rs.at[z - t], dev_r).wait_recv()
+
+                @pl.when(z < nz - 1)
+                def _():
+                    if t < nz - 1:
+                        right(t).start()
+
+            @pl.when(z + t < nz)
+            def _():
+                if t > 0:
+                    rc(at(z + t), at(z + t), ss.at[1, 0], rs.at[z + t], dev_l).wait_recv()
+
+                @pl.when(z > 0)
+                def _():
+                    if t < nz - 1:
+                        left(t).start()
+
+        def drain():
+            for t in range(nz - 1):
+                @pl.when((z - t >= 0) & (z < nz - 1))
+                def _():
+                    right(t).wait_send()
+
+                @pl.when((z + t < nz) & (z > 0))
+                def _():
+                    left(t).wait_send()
+
+        return step, drain
+
     nch = ld.shape[1]
     ch = rows // nch
 
@@ -70,8 +111,11 @@
     for i in range(nch):
         for c in loads(i):
             c.start()
-    own_m = pltpu.make_async_copy(mix_ref, mg.at[gc, g], mloc)
-    own_m.start()
+    hr = br // 2
+    own_m = (pltpu.make_async_copy(mix_ref.at[:hr], ma.at[core, g, z], mloc.at[0]),
+             pltpu.make_async_copy(mix_ref.at[hr:], mb.at[core, z, g], mloc.at[1]))
+    for c in own_m:
+        c.start()
 
     barrier = pltpu.get_barrier_semaphore()
     for k in range(1, n_gcol):
@@ -81,8 +125,13 @@
         pl.semaphore_signal(barrier, inc=1, device_id=dev, device_id_type=pl.DeviceIdType.MESH)
     pl.semaphore_wait(barrier, n_gcol - 1 + 2)
 
-    m_1 = rc(mix_ref, mg.at[gc, g], m1s, m1r, dev_1)
-    m_1.start()
+    for c in own_m:
+        c.wait()
+    a_step, a_drain = line(lambda i: ma.at[core, g, i], azs, azr)
+    b_step, b_drain = line(lambda i: mb.at[core, i], bzs, bzr)
+    b_1 = rc(mb.at[core, z, g], mb.at[core, z, g], b1s, b1r, dev_1)
+    b_1.start()
+    a_step(0)
 
     kt = jnp.transpose(jnp.broadcast_to(kin_ref[...], (128, rows)))
     for i in range(nch):
@@ -108,12 +157,12 @@
                         pth[k, o:o + 128, r] = jnp.transpose(xhi)
                         ptl[k, o:o + 128, r] = jnp.transpose(xlo)
 
-    own_m.wait()
-    m_1.wait()
-    mg_1 = [rc(mg.at[gc, gx], mg.at[gc, gx], m2s.at[k], m2r.at[k], dev_2)
-            for k, gx in enumerate((g, g1))]
-    for c in mg_1:
-        c.start()
+    b_1.wait()
+    b_2 = [rc(mb.at[core, z, gx], mb.at[core, z, gx], b2s.at[k], b2r.at[k], dev_2)
+           for k, gx in enumerate((g, g1))]
+    for c in b_2:
+        c.start()
+    a_step(1)
 
     def mm1(cx, ax):
         k = cx * 2 + ax
@@ -124,59 +173,23 @@
             out = dot3(pth[k], ptl[k], hh[:, n], hl[:, n])
             part[cx, ax, :, :, :, n] = out.reshape(2, nz, each, TN)
 
-    def line(at, ss, rs):
-        def right(t):
-            return rc(at(z - t), at(z - t), ss.at[0, t], rs.at[z - t], dev_r)
-
-        def left(t):
-            return rc(at(z + t), at(z + t), ss.at[1, t], rs.at[z + t], dev_l)
-
-        def step(t):
-            @pl.when(z - t >= 0)
-            def _():
-                if t > 0:
-                    rc(at(z - t), at(z - t), ss.at[0, 0], rs.at[z - t], dev_r).wait_recv()
-
-                @pl.when(z < nz - 1)
-                def _():
-                    if t < nz - 1:
-                        right(t).start()
-
-            @pl.when(z + t < nz)
-            def _():
-                if t > 0:
-                    rc(at(z + t), at(z + t), ss.at[1, 0], rs.at[z + t], dev_l).wait_recv()
-
-                @pl.when(z > 0)
-                def _():
-                    if t < nz - 1:
-                        left(t).start()
-
-        def drain():
-            for t in range(nz - 1):
-                @pl.when((z - t >= 0) & (z < nz - 1))
-                def _():
-                    right(t).wait_send()
-
-                @pl.when((z + t < nz) & (z > 0))
-                def _():
-                    left(t).wait_send()
-
-        return step, drain
-
-    m_step, m_drain = line(lambda i: mg.at[2 * i + core], mzs, mzr)
-
-    s0 = []
-    for i, ax in enumerate((1 - ap, ap)):
-        mm1(pc, ax)
+    def s0_send(i, ax):
         c = rc(part.at[pc, ax], r0.at[i], s0s.at[i], s0r.at[i], dev_c)
         c.start()
-        s0.append(c)
-        if i == 0:
-            for c in mg_1:
-                c.wait()
-            m_step(0)
-
+        return c
+
+    def m_core(i, ref):
+        c = rc(ref, ref, mcs.at[i], mcr.at[i], dev_c)
+        c.start()
+        return c
+
+    mm1(pc, 1 - ap)
+    s0 = [s0_send(0, 1 - ap)]
+    for c in b_2:
+        c.wait()
+    b_step(0)
+    for t in range(2, nz - 1):
+        a_step(t)
     mm1(core, 1 - a)
     s0[0].wait_recv()
     s1 = []
@@ -185,19 +198,30 @@
         c = rc(part.at[core, 1 - a, bx], r1.at[i], s1s.at[i], s1r.at[i], dev_1)
         c.start()
         s1.append(c)
+    mm1(pc, ap)
+    s0.append(s0_send(1, ap))
+    a_step(nz - 1)
+    a_1 = rc(ma.at[core, g], ma.at[core, g], a1s, a1r, dev_1)
+    a_1.start()
     mm1(core, a)
     s0[1].wait_recv()
     for bx in range(2):
         part[core, a, bx] = part[core, a, bx] + r0[1, bx]
-    m_step(1)
     s1[0].wait_recv()
     part[core, a, 1 - b] = part[core, a, 1 - b] + r1[0]
     s2 = rc(part.at[core, a, 1 - b], r2, s2s, s2r, dev_2)
     s2.start()
+    b_step(1)
     s1[1].wait_recv()
     part[core, a, b] = part[core, a, b] + r1[1]
+    a_1.wait_recv()
+    a_2 = [rc(ma.at[core, gx], ma.at[core, gx], a2s.at[k], a2r.at[k], dev_2)
+           for k, gx in enumerate((g, g1))]
+    for c in a_2:
+        c.start()
+    mc = [m_core(0, ma.at[core, g]), m_core(1, ma.at[core, g1])]
     for t in range(2, nz - 1):
-        m_step(t)
+        b_step(t)
     s2.wait_recv()
     part[core, a, b] = part[core, a, b] + r2[...]
 
@@ -247,22 +271,27 @@
     own_p = pltpu.make_async_copy(pin.at[gc], proj_ref.at[pl.ds(row0, each)], ploc)
     own_p.start()
 
-    m_step(nz - 1)
-    mc = []
+    b_step(nz - 1)
     for i in range(nz):
-        c = rc(mg.at[2 * i + core], mg.at[2 * i + core], mcs.at[i], mcr.at[i], dev_c)
-        c.start()
-        mc.append(c)
+        mc.append(m_core(n_grow + i, mb.at[core, i]))
+    for k, (c, gx) in enumerate(zip(a_2, (g, g1))):
+        c.wait_recv()
+        far = gx + w2 * (1 - 2 * b)
+        mc.append(m_core(2 + k, ma.at[core, far]))
+    for i in range(n_grow):
+        rc(ma.at[pc, i], ma.at[pc, i], mcs.at[i], mcr.at[i], dev_c).wait_recv()
     for i in range(nz):
-        rc(mg.at[2 * i + pc], mg.at[2 * i + pc], mcs.at[i], mcr.at[i], dev_c).wait_recv()
-
-    @pl.loop(0, n_gcol)
-    def _(k):
-        n = pl.ds(pl.multiple_of(k * bc, bc), bc)
-        for gx in range(n_grow):
-            hi, lo = split(mg[k, gx])
-            mh[gx * br:(gx + 1) * br, n] = hi
-            ml[gx * br:(gx + 1) * br, n] = lo
+        rc(mb.at[pc, i], mb.at[pc, i], mcs.at[n_grow + i], mcr.at[n_grow + i], dev_c).wait_recv()
+
+    for cx in range(2):
+        @pl.loop(0, nz)
+        def _(k):
+            n = pl.ds(pl.multiple_of((2 * k + cx) * bc, bc), bc)
+            for gx in range(n_grow):
+                for src, r in ((ma.at[cx, gx, k], gx * br), (mb.at[cx, k, gx], gx * br + hr)):
+                    hi, lo = split(src[...])
+                    mh[r:r + hr, n] = hi
+                    ml[r:r + hr, n] = lo
 
     ph, plo = split(pown[...])
 
@@ -334,11 +363,12 @@
            {"grow": g, "gcol": src}).wait_recv()
         sends[k - 1].wait_send()
     own_p.wait()
-    for c in mc + s0 + s1 + [s2, q2] + q1:
+    for c in mc + s0 + s1 + [s2, q2, a_1] + a_2 + q1:
         c.wait_send()
     for i in range(4):
         qc(i, core, *mine[i]).wait_send()
-    m_drain()
+    a_drain()
+    b_drain()
     q_drain()
     for t in range(nz - 1):
         @pl.when(nz - 1 - t > z)
@@ -364,7 +394,7 @@
     V = pltpu.VMEM
     return pl.pallas_call(
         functools.partial(kernel, nz, scale),
-        out_shape=(jax.ShapeDtypeStruct((rows, nb), F32), jax.ShapeDtypeStruct((br, bc), F32)),
+        out_shape=(V((rows, nb), F32), V((br, bc), F32)),
         in_specs=[pl.BlockSpec(memory_space=pl.ANY), pl.BlockSpec(memory_space=pl.ANY),
                   pl.BlockSpec(memory_space=pltpu.VMEM), pl.BlockSpec(memory_space=pltpu.VMEM)],
         out_specs=(pl.BlockSpec(memory_space=pltpu.VMEM), pl.BlockSpec(memory_space=pltpu.VMEM)),
@@ -377,16 +407,18 @@
             V((2, 2, 2, nz, each, nb), F32), V((2, 2, nz, each, nb), F32),
             V((2, nz, each, nb), F32), V((nz, each, nb), F32),
             V((nz, each, nb), F32), V((nz, each, nb), F32),
-            V((n_gcol, n_grow, br, bc), F32),
+            V((2, n_grow, nz, br // 2, bc), F32), V((2, nz, n_grow, br // 2, bc), F32),
             V((2, 2, 2, nz, each, nb), F32),
             V((each, nb), F32), V((n_gcol, each, bc), F32),
-            D((2, nch)), D, D, D((2,)), D((2,)), D((2, nz)), D((nz,)), D((nz,)), D((nz,)), D,
+            D((2, nch)), D((2,)), D((2, nz)), D((nz,)), D, D, D((2,)), D((2,)),
+            D, D, D((2,)), D((2,)), D((2, nz)), D((nz,)),
+            D((n_grow + nz,)), D((n_grow + nz,)),
             D((2,)), D((2,)), D((2,)), D((2,)), D, D, D((2, nz)), D((nz,)), D((nz,)),
             D((n_gcol,)), D((n_gcol,)), D,
             D((2, nz)), D((nz,)), D, D, D((2,)), D((2,)), D((4,)), D((4,)),
         ],
         compiler_params=pltpu.CompilerParams(
-            collective_id=0, has_side_effects=True, vmem_limit_bytes=67043328),
+            collective_id=0, has_side_effects=True, vmem_limit_bytes=52 * 2**20),
     )(psi, vpsi, kinetic.reshape(1, rows), mixing)
 
 

time: 129 us -> 121 us (0.938)
  Pallas kernels: 123 us -> 118 us
  local copies, waits for them, and re-layouts: 5.48 us -> 2.67 us
    pallas_call x1, Pallas kernels: 123 us -> 118 us  [body_kernel(): pl.pallas_call(functools.partial(kernel, nz, scale), out_shape=(V((rows,...]
    unnamed x4 -> x2, local copies, waits for them, and re-layouts: 5.48 us -> 2.67 us
where the time goes in v2:
time: 121 us
  Pallas kernels  118 us (98%)
  local copies, waits for them, and re-layouts  2.67 us (2%)
    pallas_call x1, Pallas kernels, body_kernel(): pl.pallas_call(functools.partial(kernel, nz, scale), out_shape=(V((rows,...  118 us
    unnamed x2, local copies, waits for them, and re-layouts  2.67 us

profile of v2, /device:TPU:0, one launch (start us, length us, event | category | flops | bytes accessed | tf_op | source)
XLA Modules:
  0.0 121.0 jit_solution(11577608271096651499)
XLA Ops:
  0.6 117.7 %shard_map.59 = (f32[1024,1024]{1,0:T(8,128)S(1)}, f32[256,128]{1,0:T(8,128)S(1)}) custom-call(f32[1024,1024]{1,0:T(8,128)} %psi_hbm.1, f32[1024,1024]{1,0:T(8,128)} %vpsi_hbm.1, f32[1,1024]{1,0:T(1,128)} %bitcast.1, f32[256,128]{1,0:T(8,128)} %mix_ref.1), custom_call_target="tpu_custom_call" | custom-call | tf_op jit(solution)/shard_map/pallas_call | solution.py:395
  118.3 2.0 %copy.8 = f32[1024,1024]{1,0:T(8,128)} copy(f32[1024,1024]{1,0:T(8,128)S(1)} %get-tuple-element.2) | data formatting | bytes 8388608
  120.3 0.7 copy.9

commit v3 on v2

--- a/solution.py
+++ b/solution.py
@@ -203,6 +203,7 @@
     a_step(nz - 1)
     a_1 = rc(ma.at[core, g], ma.at[core, g], a1s, a1r, dev_1)
     a_1.start()
+    b_step(1)
     mm1(core, a)
     s0[1].wait_recv()
     for bx in range(2):
@@ -211,49 +212,44 @@
     part[core, a, 1 - b] = part[core, a, 1 - b] + r1[0]
     s2 = rc(part.at[core, a, 1 - b], r2, s2s, s2r, dev_2)
     s2.start()
-    b_step(1)
+    for t in range(2, nz - 1):
+        b_step(t)
     s1[1].wait_recv()
     part[core, a, b] = part[core, a, b] + r1[1]
-    a_1.wait_recv()
-    a_2 = [rc(ma.at[core, gx], ma.at[core, gx], a2s.at[k], a2r.at[k], dev_2)
-           for k, gx in enumerate((g, g1))]
-    for c in a_2:
-        c.start()
-    mc = [m_core(0, ma.at[core, g]), m_core(1, ma.at[core, g1])]
-    for t in range(2, nz - 1):
-        b_step(t)
     s2.wait_recv()
     part[core, a, b] = part[core, a, b] + r2[...]
 
-    def zr(t):
-        d = nz - 1 - t
-        return rc(part.at[core, a, b, d], rzr.at[d], zs.at[0, t], zrr.at[d], dev_r)
-
-    def zl(t):
-        return rc(part.at[core, a, b, t], rzl.at[t], zs.at[1, t], zrl.at[t], dev_l)
-
-    for t in range(nz):
-        d = nz - 1 - t
-
-        @pl.when((z > 0) & (d >= z))
-        def _():
-            rc(part.at[core, a, b, d], rzr.at[d], zs.at[0, 0], zrr.at[d], dev_r).wait_recv()
-            part[core, a, b, d] = part[core, a, b, d] + rzr[d]
-
-        if t < nz - 1:
-            @pl.when(d > z)
-            def _():
-                zr(t).start()
-
-        @pl.when((z < nz - 1) & (t <= z))
-        def _():
-            rc(part.at[core, a, b, t], rzl.at[t], zs.at[1, 0], zrl.at[t], dev_l).wait_recv()
-            part[core, a, b, t] = part[core, a, b, t] + rzl[t]
-
-        if t < nz - 1:
-            @pl.when(t < z)
-            def _():
-                zl(t).start()
+    def zsum(buf, ss, rs, dev, d):
+        return rc(part.at[core, a, b, d], buf.at[d], ss, rs.at[d], dev)
+
+    for tick in range(2 * nz - 1):
+        if tick == 1:
+            a_1.wait_recv()
+            a_2 = [rc(ma.at[core, gx], ma.at[core, gx], a2s.at[k], a2r.at[k], dev_2)
+                   for k, gx in enumerate((g, g1))]
+            for c in a_2:
+                c.start()
+            mc = [m_core(0, ma.at[core, g]), m_core(1, ma.at[core, g1])]
+        dr = nz - 1 - (tick - z)
+        dl = tick - (nz - 1 - z)
+
+        @pl.when((dr <= nz - 1) & (dr >= z) & (z > 0))
+        def _():
+            zsum(rzr, zs.at[0, 0], zrr, dev_r, dr).wait_recv()
+            part[core, a, b, dr] = part[core, a, b, dr] + rzr[dr]
+
+        @pl.when((dr <= nz - 1) & (dr > z))
+        def _():
+            zsum(rzr, zs.at[0, dr], zrr, dev_r, dr).start()
+
+        @pl.when((dl >= 0) & (dl <= z) & (z < nz - 1))
+        def _():
+            zsum(rzl, zs.at[1, 0], zrl, dev_l, dl).wait_recv()
+            part[core, a, b, dl] = part[core, a, b, dl] + rzl[dl]
+
+        @pl.when((dl >= 0) & (dl < z))
+        def _():
+            zsum(rzl, zs.at[1, dl], zrl, dev_l, dl).start()
 
     own = part[core, a, b, z] * scale
     pown[...] = own
@@ -370,14 +366,14 @@
     a_drain()
     b_drain()
     q_drain()
-    for t in range(nz - 1):
-        @pl.when(nz - 1 - t > z)
-        def _():
-            zr(t).wait_send()
-
-        @pl.when(t < z)
-        def _():
-            zl(t).wait_send()
+    for d in range(nz):
+        @pl.when(d > z)
+        def _():
+            zsum(rzr, zs.at[0, d], zrr, dev_r, d).wait_send()
+
+        @pl.when(d < z)
+        def _():
+            zsum(rzl, zs.at[1, d], zrl, dev_l, d).wait_send()
 
 
 def body_kernel(psi, vpsi, kinetic, mixing):

time: 121 us -> 97.6 us (0.81)
  Pallas kernels: 118 us -> 94.1 us
    pallas_call x1, Pallas kernels: 118 us -> 94.1 us  [body_kernel(): pl.pallas_call(functools.partial(kernel, nz, scale), out_shape=(V((rows,...]
where the time goes in v3:
time: 97.6 us; the launch traced here: 97.4 us
  Pallas kernels  94.1 us (96%)
  local copies, waits for them, and re-layouts  2.67 us (3%)
    pallas_call x1, Pallas kernels, body_kernel(): pl.pallas_call(functools.partial(kernel, nz, scale), out_shape=(V((rows,...  94.1 us
    unnamed x2, local copies, waits for them, and re-layouts  2.67 us

profile of v3, /device:TPU:0, one launch (start us, length us, event | category | flops | bytes accessed | tf_op | source)
XLA Modules:
  0.0 97.4 jit_solution(2084746689593067062)
XLA Ops:
  0.6 94.1 %shard_map.59 = (f32[1024,1024]{1,0:T(8,128)S(1)}, f32[256,128]{1,0:T(8,128)S(1)}) custom-call(f32[1024,1024]{1,0:T(8,128)} %psi_hbm.1, f32[1024,1024]{1,0:T(8,128)} %vpsi_hbm.1, f32[1,1024]{1,0:T(1,128)} %bitcast.1, f32[256,128]{1,0:T(8,128)} %mix_ref.1), custom_call_target="tpu_custom_call" | custom-call | tf_op jit(solution)/shard_map/pallas_call | solution.py:391
  94.7 2.0 %copy.8 = f32[1024,1024]{1,0:T(8,128)} copy(f32[1024,1024]{1,0:T(8,128)S(1)} %get-tuple-element.2) | data formatting | bytes 8388608
  96.7 0.7 copy.9

commit v4 on v3

--- a/solution.py
+++ b/solution.py
@@ -28,7 +28,8 @@
            ld, mloc, azs, azr, a1s, a1r, a2s, a2r, b1s, b1r, b2s, b2r, bzs, bzr,
            mcs, mcr,
            s0s, s0r, s1s, s1r, s2s, s2r, zs, zrr, zrl, ps, pr, ploc,
-           qzs, qzr, q2s, q2r, q1s, q1r, qcs, qcr):
+           qzs, qzr, q2s, q2r, q1s, q1r, qcs, qcr,
+           e1s, e1r, e2s, e2r, ezs, ezr, ecs, ecr):
     rows, nb = psi_v.shape
     n_grow = mb.shape[2]
     n_gcol = 2 * nz
@@ -296,7 +297,11 @@
         n = pl.ds(pl.multiple_of(j * TN, TN), TN)
         q[core, a, b, z, :, n] = dot3(ph, plo, mh[:, n], ml[:, n])
 
-    q_step, q_drain = line(lambda i: q.at[core, a, b, i], qzs, qzr)
+    cut = nb - (3 * nb // 8) // 128 * 128
+    A = slice(0, cut)
+    B = slice(cut, nb)
+    q_step, q_drain = line(lambda i: q.at[core, a, b, i, :, A], qzs, qzr)
+    e_step, e_drain = line(lambda i: q.at[core, :, :, i, :, B], ezs, ezr)
 
     def hmix(i):
         @pl.loop(0, nb // TN)
@@ -305,52 +310,84 @@
             r = slice(i * (rows // 4), (i + 1) * (rows // 4))
             res_ref[r, n] = dot3(hh[r, :], hl[r, :], mh[:, n], ml[:, n])
 
-    def finish(cx, ax):
+    def finish(cx, ax, n):
         k = cx * 2 + ax
-
-        @pl.loop(0, nb // TN)
-        def _(j):
-            n = pl.ds(pl.multiple_of(j * TN, TN), TN)
-            qh, ql = split(q[cx, ax, :, :, :, n].reshape(grp, TN))
-            for i in range(4):
-                r = slice(i * (rows // 4), (i + 1) * (rows // 4))
-                res_ref[r, n] = res_ref[r, n] - dot3(psh[k, r, :], psl[k, r, :], qh, ql)
+        qh, ql = split(q[cx, ax, :, :, :, n].reshape(grp, n.stop - n.start))
+        for i in range(4):
+            r = slice(i * (rows // 4), (i + 1) * (rows // 4))
+            res_ref[r, n] = res_ref[r, n] - dot3(psh[k, r, :], psl[k, r, :], qh, ql)
 
     def qc(i, cx, ax, bx):
-        return rc(q.at[cx, ax, bx], q.at[cx, ax, bx], qcs.at[i], qcr.at[i], dev_c)
+        at = q.at[cx, ax, bx, :, :, A]
+        return rc(at, at, qcs.at[i], qcr.at[i], dev_c)
+
+    def ec(i, cx):
+        at = q.at[cx, :, :, i, :, B]
+        return rc(at, at, ecs.at[i], ecr.at[i], dev_c)
+
+    def q_send(ax, bx, ss, rs, dev):
+        at = q.at[core, ax, bx, :, :, A]
+        return rc(at, at, ss, rs, dev)
+
+    def e_send(ax, ss, rs, dev):
+        at = q.at[core, ax, b, z, :, B]
+        return rc(at, at, ss, rs, dev)
 
     mine = ((a, b), (a, 1 - b), (1 - a, b), (1 - a, 1 - b))
     other = ((ap, bp), (ap, 1 - bp), (1 - ap, bp), (1 - ap, 1 - bp))
 
+    e1 = e_send(a, e1s, e1r, dev_1)
+    e1.start()
     q_step(0)
     hmix(0)
-    for t in range(1, nz):
+    e1.wait_recv()
+    e2 = [e_send(ax, e2s.at[i], e2r.at[i], dev_2) for i, ax in enumerate((a, 1 - a))]
+    for c in e2:
+        c.start()
+    q_step(1)
+    hmix(1)
+    for t in range(2, nz - 1):
         q_step(t)
-        if t < min(4, nz - 1):
-            hmix(t)
-    q2 = rc(q.at[core, a, b], q.at[core, a, b], q2s, q2r, dev_2)
+    for c in e2:
+        c.wait_recv()
+    e_step(0)
+    hmix(2)
+    q_step(nz - 1)
+    q2 = q_send(a, b, q2s, q2r, dev_2)
     q2.start()
-    q1 = [rc(q.at[core, a, b], q.at[core, a, b], q1s.at[0], q1r.at[0], dev_1),
-          rc(q.at[core, a, 1 - b], q.at[core, a, 1 - b], q1s.at[1], q1r.at[1], dev_1)]
+    q1 = [q_send(a, b, q1s.at[0], q1r.at[0], dev_1),
+          q_send(a, 1 - b, q1s.at[1], q1r.at[1], dev_1)]
     q1[0].start()
     qc(0, core, *mine[0]).start()
-    for i in range(min(4, nz - 1), 4):
-        hmix(i)
-    rc(q.at[core, a, 1 - b], q.at[core, a, 1 - b], q2s, q2r, dev_2).wait_recv()
+    hmix(3)
+    e_step(1)
+    q_send(a, 1 - b, q2s, q2r, dev_2).wait_recv()
     q1[1].start()
     qc(1, core, *mine[1]).start()
-    finish(core, a)
+    for t in range(2, nz - 1):
+        e_step(t)
+    finish(core, a, A)
     qc(0, pc, *other[0]).wait_recv()
     qc(1, pc, *other[1]).wait_recv()
-    finish(pc, ap)
-    rc(q.at[core, 1 - a, b], q.at[core, 1 - a, b], q1s.at[0], q1r.at[0], dev_1).wait_recv()
+    finish(pc, ap, A)
+    e_step(nz - 1)
+    ecs_own = [ec(i, core) for i in range(nz)]
+    for c in ecs_own:
+        c.start()
+    q_send(1 - a, b, q1s.at[0], q1r.at[0], dev_1).wait_recv()
     qc(2, core, *mine[2]).start()
-    rc(q.at[core, 1 - a, 1 - b], q.at[core, 1 - a, 1 - b], q1s.at[1], q1r.at[1], dev_1).wait_recv()
+    finish(core, 0, B)
+    q_send(1 - a, 1 - b, q1s.at[1], q1r.at[1], dev_1).wait_recv()
     qc(3, core, *mine[3]).start()
-    finish(core, 1 - a)
+    finish(core, 1, B)
+    finish(core, 1 - a, A)
+    for i in range(nz):
+        ec(i, pc).wait_recv()
+    finish(pc, 0, B)
+    finish(pc, 1, B)
     qc(2, pc, *other[2]).wait_recv()
     qc(3, pc, *other[3]).wait_recv()
-    finish(pc, 1 - ap)
+    finish(pc, 1 - ap, A)
 
     for k in range(1, n_gcol):
         src = lax.rem(gc + n_gcol - k, n_gcol)
@@ -359,13 +396,14 @@
            {"grow": g, "gcol": src}).wait_recv()
         sends[k - 1].wait_send()
     own_p.wait()
-    for c in mc + s0 + s1 + [s2, q2, a_1] + a_2 + q1:
+    for c in mc + s0 + s1 + [s2, q2, a_1, e1] + a_2 + q1 + e2 + ecs_own:
         c.wait_send()
     for i in range(4):
         qc(i, core, *mine[i]).wait_send()
     a_drain()
     b_drain()
     q_drain()
+    e_drain()
     for d in range(nz):
         @pl.when(d > z)
         def _():
@@ -412,6 +450,7 @@
             D((2,)), D((2,)), D((2,)), D((2,)), D, D, D((2, nz)), D((nz,)), D((nz,)),
             D((n_gcol,)), D((n_gcol,)), D,
             D((2, nz)), D((nz,)), D, D, D((2,)), D((2,)), D((4,)), D((4,)),
+            D, D, D((2,)), D((2,)), D((2, nz)), D((nz,)), D((nz,)), D((nz,)),
         ],
         compiler_params=pltpu.CompilerParams(
             collective_id=0, has_side_effects=True, vmem_limit_bytes=52 * 2**20),

time: 97.6 us -> 90.3 us (0.925)
  Pallas kernels: 94.1 us -> 86.1 us
    pallas_call x1, Pallas kernels: 94.1 us -> 86.1 us  [body_kernel(): pl.pallas_call(functools.partial(kernel, nz, scale), out_shape=(V((rows,...]
where the time goes in v4:
time: 90.3 us; the launch traced here: 89.4 us
  Pallas kernels  86.1 us (95%)
  local copies, waits for them, and re-layouts  2.67 us (3%)
    pallas_call x1, Pallas kernels, body_kernel(): pl.pallas_call(functools.partial(kernel, nz, scale), out_shape=(V((rows,...  86.1 us
    unnamed x2, local copies, waits for them, and re-layouts  2.67 us

profile of v4, /device:TPU:0, one launch (start us, length us, event | category | flops | bytes accessed | tf_op | source)
XLA Modules:
  0.0 89.4 jit_solution(12800170203653217437)
XLA Ops:
  0.6 86.1 %shard_map.59 = (f32[1024,1024]{1,0:T(8,128)S(1)}, f32[256,128]{1,0:T(8,128)S(1)}) custom-call(f32[1024,1024]{1,0:T(8,128)} %psi_hbm.1, f32[1024,1024]{1,0:T(8,128)} %vpsi_hbm.1, f32[1,1024]{1,0:T(1,128)} %bitcast.1, f32[256,128]{1,0:T(8,128)} %mix_ref.1), custom_call_target="tpu_custom_call" | custom-call | tf_op jit(solution)/shard_map/pallas_call | solution.py:429
  86.8 2.0 %copy.8 = f32[1024,1024]{1,0:T(8,128)} copy(f32[1024,1024]{1,0:T(8,128)S(1)} %get-tuple-element.2) | data formatting | bytes 8388608
  88.8 0.7 copy.9
